TPU v7x, 128 devices: a whole 4x4x4 slice. The times are simulated.
128 devices in a mesh: row: 16 (over z_hi, x, core), col: 8 (over y, z_lo).
Axes of the slice: x: 4, y: 4, z: 4 (z_hi: 2, z_lo: 2; z = z_hi * 2 + z_lo), core: 2. Of those that a mesh axis runs over, the one named last changes fastest.
Arguments:
- pair: bfloat16 [512, 512, 128], P('row', 'col'), may hold values from -6 to 6
- cotangent: bfloat16 [512, 512, 128], P('row', 'col'), may hold values from -6 to 6
- length: int32 [1], replicated, may hold values from 256 to 512
- norm_gain: float32 [128], replicated, may hold values from 0.1 to 1.9
- norm_bias: float32 [128], replicated, may hold values from -1.5 to 1.5
- left_weight: bfloat16 [128, 256], replicated, may hold values from -0.5 to 0.5
- right_weight: bfloat16 [128, 256], replicated, may hold values from -0.5 to 0.5
- gate_weight: bfloat16 [128, 128], replicated, may hold values from -0.5 to 0.5
- out_gain: float32 [128], replicated, may hold values from 0.1 to 1.9
- out_bias: float32 [128], replicated, may hold values from -2 to 2
- out_weight: bfloat16 [128, 128], replicated, may hold values from -0.5 to 0.5
Outputs:
- update: bfloat16 [512, 512, 128], P('row', 'col')
- grad_pair: bfloat16 [512, 512, 128], P('row', 'col')
- grad_left: float32 [128, 256], replicated
- grad_right: float32 [128, 256], replicated
- grad_gating: float32 [128, 128], replicated
- grad_output: float32 [128, 128], replicated
- grad_norms: float32 [4, 128], replicated
Inputs may be any that keep to these rules, and one draw needn't show every extreme that they name: Tokens at positions 511 down to length are padding.
All inputs are finite; a program needn't handle non-finite values.
Results may differ from a plain program's by a relative error of at most 0.014.
Values may be sent and summed in bfloat16 or wider, within the bound.
A program may use at most 128 MiB of HBM per device.

v0:
```python
import jax
import jax.numpy as jnp
from jax import lax
from jax.sharding import PartitionSpec as P

EPS = 1e-05
AXES = ("row", "col")


def normalize(values):
    center = values - jnp.mean(values, axis=-1, keepdims=True)
    inverse = lax.rsqrt(jnp.mean(center * center, axis=-1, keepdims=True) + EPS)
    return (center * inverse, inverse)


def exchange(x):
    return lax.all_to_all(x, AXES, 0, 0, tiled=True)


def per_device(
    pair,
    cotangent,
    length,
    norm_gain,
    norm_bias,
    left_weight,
    right_weight,
    gate_weight,
    out_gain,
    out_bias,
    out_weight,
):
    n_row = lax.axis_size("row")
    n_col = lax.axis_size("col")
    n = n_row * n_col
    rows, cols = pair.shape[:2]
    tokens = rows * n_row
    hidden = out_weight.shape[0]
    row_at = lax.axis_index("row") * rows
    col_at = lax.axis_index("col") * cols
    first_ok = row_at + jnp.arange(rows, dtype=jnp.int32) < length[0]
    second_ok = col_at + jnp.arange(cols, dtype=jnp.int32) < length[0]
    mask = (first_ok[:, None] & second_ok[None, :]).astype(jnp.float32).reshape(1, -1)

    def to_owner(tiles):
        return exchange(jnp.stack([t.reshape(n, rows * cols // 128, 128) for t in tiles], axis=1))

    def whole(received):
        return (
            received.reshape(n_row, n_col, rows, cols).transpose(0, 2, 1, 3).reshape(tokens, tokens)
        )

    def tiled(matrix):
        t = matrix.reshape(n_row, rows, n_col, cols).transpose(0, 2, 1, 3)
        return t.reshape(n, rows * cols // 128, 128)

    pair_hat, pair_scale = normalize(pair.astype(jnp.float32))
    normed = (pair_hat * norm_gain + norm_bias).astype(jnp.bfloat16)
    flat = normed.reshape(rows * cols, -1)

    def dot(form, a, b):
        return jnp.einsum(form, a, b, preferred_element_type=jnp.float32)

    def gating(weight):
        projected = dot("pc,ch->hp", flat, weight)
        values = projected[:hidden]
        sig = jax.nn.sigmoid(projected[hidden:])
        return ((mask * sig * values).astype(jnp.bfloat16), values, sig)

    left, left_val, left_sig = gating(left_weight)
    right, right_val, right_sig = gating(right_weight)
    got = to_owner([left, right])
    big_l = whole(got[:, 0])
    big_r = whole(got[:, 1])
    tri_own = dot("ik,jk->ij", big_l, big_r).astype(jnp.bfloat16)
    tri = exchange(tiled(tri_own)).reshape(hidden, -1).astype(jnp.float32)
    center = tri - jnp.mean(tri, axis=0, keepdims=True)
    tri_scale = lax.rsqrt(jnp.mean(center * center, axis=0, keepdims=True) + EPS)
    tri_hat = center * tri_scale
    tri_normed = (tri_hat * out_gain[:, None] + out_bias[:, None]).astype(jnp.bfloat16)
    outer = dot("hp,hc->cp", tri_normed, out_weight)
    gate = jax.nn.sigmoid(dot("pc,cd->dp", flat, gate_weight))
    update = (gate * outer).astype(jnp.bfloat16).T.reshape(pair.shape)
    upstream = cotangent.reshape(rows * cols, -1).T.astype(jnp.float32)
    outer_grad = (upstream * gate).astype(jnp.bfloat16)
    gate_grad = (upstream * outer * gate * (1.0 - gate)).astype(jnp.bfloat16)
    grad_output = dot("hp,cp->hc", tri_normed, outer_grad)
    grad_gating = dot("pc,dp->cd", flat, gate_grad)
    tnorm_grad = dot("cp,hc->hp", outer_grad, out_weight)
    hat_grad = tnorm_grad * out_gain[:, None]
    tri_grad = (
        tri_scale
        * (
            hat_grad
            - jnp.mean(hat_grad, axis=0, keepdims=True)
            - tri_hat * jnp.mean(hat_grad * tri_hat, axis=0, keepdims=True)
        )
    ).astype(jnp.bfloat16)
    g = whole(exchange(tri_grad.reshape(n, rows * cols // 128, 128)))
    row_own = dot("ij,jk->ik", g, big_r).astype(jnp.bfloat16)
    col_own = dot("ij,ik->jk", g, big_l).astype(jnp.bfloat16)
    back = exchange(jnp.stack([tiled(row_own), tiled(col_own)], axis=1))
    row_part = back[:, 0].reshape(hidden, -1).astype(jnp.float32)
    col_part = back[:, 1].reshape(hidden, -1).astype(jnp.float32)

    def push_back(part, values, sig, weight):
        comb = jnp.concatenate(
            [part * mask * sig, part * mask * values * sig * (1.0 - sig)], axis=0
        ).astype(jnp.bfloat16)
        return (dot("hp,ch->pc", comb, weight), dot("pc,hp->ch", flat, comb))

    from_rows, grad_left = push_back(row_part, left_val, left_sig, left_weight)
    from_cols, grad_right = push_back(col_part, right_val, right_sig, right_weight)
    gate_back = dot("dp,cd->pc", gate_grad, gate_weight)
    normed_grad = (gate_back + from_rows + from_cols).reshape(pair.shape)
    scaled = normed_grad * norm_gain
    grad_pair = (
        pair_scale
        * (
            scaled
            - jnp.mean(scaled, axis=-1, keepdims=True)
            - pair_hat * jnp.mean(scaled * pair_hat, axis=-1, keepdims=True)
        )
    ).astype(jnp.bfloat16)
    grad_norms = jnp.stack(
        [
            jnp.sum(normed_grad * pair_hat, axis=(0, 1)),
            jnp.sum(normed_grad, axis=(0, 1)),
            jnp.sum(tnorm_grad * tri_hat, axis=1),
            jnp.sum(tnorm_grad, axis=1),
        ]
    )
    parts = [grad_left, grad_right, grad_gating, grad_output, grad_norms]
    flat_parts = jnp.concatenate([a.reshape(-1, 128) for a in parts], axis=0)
    size = flat_parts.shape[0]
    per = -(-size // (n * 8)) * 8
    padded = jnp.pad(flat_parts, ((0, per * n - size), (0, 0))).reshape(n, per, 128)
    mine = jnp.sum(exchange(padded), axis=0) * (1.0 / tokens)
    total = lax.all_gather(mine, AXES, axis=0, tiled=True)
    done, at = ([], 0)
    for a in parts:
        count = a.size // 128
        done.append(total[at : at + count].reshape(a.shape))
        at += count
    return (update, grad_pair, *done)


def solution(mesh):
    return jax.shard_map(
        per_device,
        mesh=mesh,
        in_specs=(P("row", "col", None), P("row", "col", None)) + (P(),) * 9,
        out_specs=(P("row", "col", None), P("row", "col", None)) + (P(),) * 5,
        check_vma=False,
    )
```

profile of v0, /device:TPU:0, one launch (start us, length us, event | category | flops | bytes accessed | tf_op | source)
XLA Modules:
  0.0 505.4 jit_solution(2819725478493641133)
XLA Ops:
  2.9 1.7 fusion.17
  4.7 1.7 fusion.11
  11.7 29.5 %all_to_all.25 = bf16[128,2,16,128]{3,2,1,0:T(8,128)(2,1)S(1)} all-to-all(bf16[128,2,16,128]{3,2,1,0:T(8,128)(2,1)S(1)} %pad_maximum_fusion), channel_id=1, replica_groups=mesh['row'=16,'col'=8] {'row','col'}, dimensions={0} | all-to-all | bytes 2097152 | tf_op jit(solution)/shard_map/all_to_all | solution.py:17
  42.3 1.6 reshape_squeeze.9
  45.4 1.9 reshape.175
  47.3 2.6 reshape_squeeze.8
  49.9 2.7 copy.34
  52.6 1.9 reshape.174
  56.5 1.6 reshape.176
  59.4 1.8 reshape.177
  61.2 18.5 %all_to_all.26 = bf16[128,16,128]{2,1,0:T(8,128)(2,1)S(1)} all-to-all(bf16[128,16,128]{2,1,0:T(8,128)(2,1)S(1)} %reshape.177), channel_id=1, replica_groups=mesh['row'=16,'col'=8] {'row','col'}, dimensions={0} | all-to-all | bytes 1048576 | tf_op jit(solution)/shard_map/all_to_all | solution.py:17
  85.4 1.7 fusion.24
  87.1 2.4 multiply_convert_fusion.4
  90.9 18.2 %all_to_all.27 = bf16[128,16,128]{2,1,0:T(8,128)(2,1)} all-to-all(bf16[128,16,128]{2,1,0:T(8,128)(2,1)S(1)} %copy.38), channel_id=1, replica_groups=mesh['row'=16,'col'=8] {'row','col'}, dimensions={0} | all-to-all | bytes 1048576 | tf_op jit(solution)/shard_map/all_to_all | solution.py:17
  109.1 1.6 reshape.180
  112.2 1.9 reshape.181
  114.2 2.3 convolution_convert_fusion
  117.7 1.6 reshape.182
  120.5 2.4 stack_reshape.14
  125.8 1.8 stack_reshape.15
  129.9 6.0 %all-to-all-start.3 = ((bf16[128,2,16,128]{3,2,1,0:T(8,128)(2,1)}), bf16[128,2,16,128]{3,2,1,0:T(8,128)(2,1)}, u32[]{:S(2)}, u32[]{:S(2)}) async-start(bf16[128,2,16,128]{3,2,1,0:T(8,128)(2,1)} %copy.42), calls=%async_computation.3 | async-start | bytes 2097152 | tf_op jit(solution)/shard_map/all_to_all | solution.py:17
  136.2 2.2 fusion.48
  138.4 2.2 fusion.47
  140.5 13.3 %all-to-all-done.3 = bf16[128,2,16,128]{3,2,1,0:T(8,128)(2,1)} async-done(((bf16[128,2,16,128]{3,2,1,0:T(8,128)(2,1)}), bf16[128,2,16,128]{3,2,1,0:T(8,128)(2,1)}, u32[]{:S(2)}, u32[]{:S(2)}) %all-to-all-start.3) | async-done | bytes 1048608 | tf_op jit(solution)/shard_map/all_to_all | solution.py:17
  153.8 2.7 slice_convert_fusion.1
  158.1 2.6 copy.44
  160.6 2.4 multiply_convert_fusion.3
  165.7 2.3 fusion.42
  170.0 5.3 %all-to-all-start.4 = ((f32[128,8,128]{2,1,0:T(8,128)}), f32[128,8,128]{2,1,0:T(8,128)S(1)}, u32[]{:S(2)}, u32[]{:S(2)}) async-start(f32[128,8,128]{2,1,0:T(8,128)} %pad_bitcast_fusion), calls=%async_computation.4 | async-start | bytes 1048576 | tf_op jit(solution)/shard_map/all_to_all | solution.py:17
  175.4 1.9 fusion.15
  177.3 11.4 %all-to-all-done.4 = f32[128,8,128]{2,1,0:T(8,128)S(1)} async-done(((f32[128,8,128]{2,1,0:T(8,128)}), f32[128,8,128]{2,1,0:T(8,128)S(1)}, u32[]{:S(2)}, u32[]{:S(2)}) %all-to-all-start.4) | async-done | bytes 524320 | tf_op jit(solution)/shard_map/all_to_all | solution.py:17
  188.8 313.9 %all_gather.3 = f32[1024,128]{1,0:T(8,128)S(1)} all-gather(f32[8,128]{1,0:T(8,128)S(1)} %broadcast_multiply_fusion.6), channel_id=1, replica_groups=mesh['row'=16,'col'=8] {'row','col'}, dimensions={0}, use_global_device_ids=true | all-gather | bytes 528384 | tf_op jit(solution)/shard_map/all_gather | solution.py:139
  (108 shorter events, 38.0 us)
Async XLA Ops:
  0.6 5.7 %copy-start = (bf16[128,256]{1,0:T(8,128)(2,1)S(1)}, bf16[128,256]{1,0:T(8,128)(2,1)}, u32[]{:S(2)}) copy-start(bf16[128,256]{1,0:T(8,128)(2,1)} %param.17) | copy-start | bytes 196612
  2.9 4.2 copy-start.18
  6.3 0.8 copy-start.6
  7.6 1.3 copy-start.1
  47.3 7.2 %copy-start.9 = (bf16[512,512]{1,0:T(8,128)(2,1)}, bf16[512,512]{1,0:T(8,128)(2,1)S(1)}, u32[]{:S(2)}) copy-start(bf16[512,512]{1,0:T(8,128)(2,1)S(1)} %reshape.175) | copy-start | bytes 1572868
  54.5 0.8 copy-start.14
  61.2 20.8 %copy-start.22 = (f32[128]{0:T(128)S(1)}, f32[128]{0:T(128)}, u32[]{:S(2)}) copy-start(f32[128]{0:T(128)} %param.19) | copy-start | bytes 1540
  61.2 20.8 %copy-start.25 = (f32[128]{0:T(128)S(1)}, f32[128]{0:T(128)}, u32[]{:S(2)}) copy-start(f32[128]{0:T(128)} %param.20) | copy-start | bytes 1540
  79.7 0.8 copy-start.5
  79.7 2.9 copy-start.19
  80.5 2.4 copy-start.20
  82.0 1.0 copy-start.7
  82.6 1.6 copy-start.13
  83.0 1.2 copy-start.15
  85.4 4.1 copy-start.11
  87.0 2.4 copy-start.3
  112.2 4.3 copy-start.10
  128.8 7.1 %copy-start.4 = (f32[2048,128]{1,0:T(8,128)S(1)}, f32[2048,128]{1,0:T(8,128)}, u32[]{:S(2)}) copy-start(f32[2048,128]{1,0:T(8,128)} %copy-done.3) | copy-start | bytes 3145732
  129.9 23.9 %all-to-all-start.3 = ((bf16[128,2,16,128]{3,2,1,0:T(8,128)(2,1)}), bf16[128,2,16,128]{3,2,1,0:T(8,128)(2,1)}, u32[]{:S(2)}, u32[]{:S(2)}) async-start(bf16[128,2,16,128]{3,2,1,0:T(8,128)(2,1)} %copy.42), calls=%async_computation.3 | async-start | bytes 2097152 | tf_op jit(solution)/shard_map/all_to_all | solution.py:17
  160.6 2.4 copy-start.8
  163.9 1.8 copy-start.12
  163.9 1.8 copy-start.21
  165.6 2.4 copy-start.2
  168.0 1.1 copy-start.16
  168.0 1.1 copy-start.17
  168.0 1.1 copy-start.23
  168.0 1.1 copy-start.24
  170.0 18.7 %all-to-all-start.4 = ((f32[128,8,128]{2,1,0:T(8,128)}), f32[128,8,128]{2,1,0:T(8,128)S(1)}, u32[]{:S(2)}, u32[]{:S(2)}) async-start(f32[128,8,128]{2,1,0:T(8,128)} %pad_bitcast_fusion), calls=%async_computation.4 | async-start | bytes 1048576 | tf_op jit(solution)/shard_map/all_to_all | solution.py:17
where the time goes:
time: 507 us; the launch traced here: 505 us
  blocking collectives  380 us (75%)
  local copies, waits for them, and re-layouts  48.8 us (10%)
  waiting for transfers between devices  24.6 us (5%)
  other arithmetic  20.7 us (4%)
  matrix products  18 us (4%)
  starting transfers between devices  11.3 us (2%)
    all_gather x1, blocking collectives, per_device(): total = lax.all_gather(mine, AXES, axis=0, tiled=True)  314 us
    all_to_all x3, blocking collectives, exchange(): return lax.all_to_all(x, AXES, 0, 0, tiled=True)  66.2 us
    all_to_all x2, waiting for transfers between devices, exchange(): return lax.all_to_all(x, AXES, 0, 0, tiled=True)  24.6 us
    dot_general x15, matrix products, dot(): return jnp.einsum(form, a, b, preferred_element_type=jnp.float32)  18 us
    all_to_all x2, starting transfers between devices, exchange(): return lax.all_to_all(x, AXES, 0, 0, tiled=True)  11.3 us
  transfers between devices with their start and end apart: 2, of which 2 were waited for; matrix products, arithmetic and copies ran while one was open for 1% of the time, Pallas kernels for 0%

commit v1 on v0

--- a/solution.py
+++ b/solution.py
@@ -136,7 +136,9 @@
     per = -(-size // (n * 8)) * 8
     padded = jnp.pad(flat_parts, ((0, per * n - size), (0, 0))).reshape(n, per, 128)
     mine = jnp.sum(exchange(padded), axis=0) * (1.0 / tokens)
-    total = lax.all_gather(mine, AXES, axis=0, tiled=True)
+    total = jnp.concatenate(
+        lax.all_to_all(jnp.stack([mine] * lax.axis_size(AXES)), AXES, 0, 0), axis=0
+    )
     done, at = ([], 0)
     for a in parts:
         count = a.size // 128

time: 507 us -> 211 us (0.42)
  blocking collectives: 380 us -> 84.7 us
    all_gather x1 -> x0, blocking collectives: 314 us -> none  [per_device(): total = lax.all_gather(mine, AXES, axis=0, tiled=True)]
    all_to_all x3 -> x4, blocking collectives: 66.2 us -> 84.7 us  [exchange(): return lax.all_to_all(x, AXES, 0, 0, tiled=True)]
    all_to_all x0 -> x1, waiting for transfers between devices: none -> 11.4 us  [per_device(): lax.all_to_all(jnp.stack([mine] * lax.axis_size(AXES)), AXES, 0, 0)]
    all_to_all x2 -> x1, waiting for transfers between devices: 24.6 us -> 13.3 us  [exchange(): return lax.all_to_all(x, AXES, 0, 0, tiled=True)]
    all_to_all x2 -> x1, starting transfers between devices: 11.3 us -> 5.96 us  [exchange(): return lax.all_to_all(x, AXES, 0, 0, tiled=True)]
  transfers between devices with their start and end apart: 2 -> 2, of which waited for: 2 -> 2; matrix products, arithmetic and copies ran while one was open for 1% -> 3% of each run, Pallas kernels for 0% -> 0%
where the time goes in v1:
time: 211 us; the launch traced here: 210 us
  blocking collectives  84.7 us (40%)
  local copies, waits for them, and re-layouts  48.9 us (23%)
  waiting for transfers between devices  24.6 us (12%)
  other arithmetic  20.7 us (10%)
  matrix products  18 us (9%)
  starting transfers between devices  10.9 us (5%)
    all_to_all x4, blocking collectives, exchange(): return lax.all_to_all(x, AXES, 0, 0, tiled=True)  84.7 us
    dot_general x15, matrix products, dot(): return jnp.einsum(form, a, b, preferred_element_type=jnp.float32)  18 us
    all_to_all x1, waiting for transfers between devices, exchange(): return lax.all_to_all(x, AXES, 0, 0, tiled=True)  13.3 us
    all_to_all x1, waiting for transfers between devices, per_device(): lax.all_to_all(jnp.stack([mine] * lax.axis_size(AXES)), AXES, 0, 0)  11.4 us
    reshape x6, local copies, waits for them, and re-layouts, tiled(): t = matrix.reshape(n_row, rows, n_col, cols).transpose(0, 2, 1, 3)  8.55 us
    reshape x4, local copies, waits for them, and re-layouts, whole(): received.reshape(n_row, n_col, rows, cols).transpose(0, 2, 1, 3)  7.37 us
    all_to_all x1, starting transfers between devices, exchange(): return lax.all_to_all(x, AXES, 0, 0, tiled=True)  5.96 us
    transpose x3, local copies, waits for them, and re-layouts, whole(): received.reshape(n_row, n_col, rows, cols).transpose(0, 2, 1, 3)  5.51 us
  transfers between devices with their start and end apart: 2, of which 2 were waited for; matrix products, arithmetic and copies ran while one was open for 3% of the time, Pallas kernels for 0%

profile of v1, /device:TPU:0, one launch (start us, length us, event | category | flops | bytes accessed | tf_op | source)
XLA Modules:
  0.0 209.6 jit_solution(9787341782227586618)
XLA Ops:
  2.9 1.7 fusion.17
  4.7 1.7 fusion.11
  11.7 29.5 %all_to_all.30 = bf16[128,2,16,128]{3,2,1,0:T(8,128)(2,1)S(1)} all-to-all(bf16[128,2,16,128]{3,2,1,0:T(8,128)(2,1)S(1)} %pad_maximum_fusion), channel_id=1, replica_groups=mesh['row'=16,'col'=8] {'row','col'}, dimensions={0} | all-to-all | bytes 2097152 | tf_op jit(solution)/shard_map/all_to_all | solution.py:17
  42.3 1.6 reshape_squeeze.9
  45.4 1.9 reshape.186
  47.3 2.6 %reshape_squeeze.8 = bf16[16,8,32,64]{3,2,1,0:T(8,128)(2,1)} reshape(bf16[128,1,16,128]{3,2,1,0:T(8,128)(2,1)} %get-tuple-element.23) | data formatting | bytes 1048576 | tf_op jit(solution)/shard_map/reshape;squeeze | solution.py:50
  49.9 2.7 %copy.34 = bf16[16,32,8,64]{3,2,1,0:T(8,128)(2,1)} copy(bf16[16,32,8,64]{3,1,2,0:T(8,128)(2,1)} %bitcast.153) | data formatting | bytes 1048576 | tf_op jit(solution)/shard_map/transpose | solution.py:50
  52.6 1.9 reshape.185
  56.5 1.6 reshape.187
  59.4 1.8 reshape.188
  61.2 18.5 %all_to_all.31 = bf16[128,16,128]{2,1,0:T(8,128)(2,1)S(1)} all-to-all(bf16[128,16,128]{2,1,0:T(8,128)(2,1)S(1)} %reshape.188), channel_id=1, replica_groups=mesh['row'=16,'col'=8] {'row','col'}, dimensions={0} | all-to-all | bytes 1048576 | tf_op jit(solution)/shard_map/all_to_all | solution.py:17
  85.4 1.7 fusion.24
  87.1 2.4 %multiply_convert_fusion.4 = bf16[128,2048]{0,1:T(8,128)(2,1)} fusion(f32[2048,128]{1,0:T(8,128)S(1)} %get-tuple-element.36, f32[128,16,128]{0,2,1:T(8,128)S(1)} %copy.37, f32[2048]{0:T(1024)S(1)} %get-tuple-element.38, f32[2048]{0:T(1024)S(1)} %get-tuple-element.39, f32[128]{0:T(128)S(1)} %copy-done.22, f32[2048]{0:T(1024)S(1)} %rsqrt_bitcast_fusion, ...), kind=kLoop, calls=%fused_computation.62 | loop fusion | flops 2097152 | bytes 2654720 | tf_op jit(solution)/shard_map/convert_element_type | solution.py:98
  90.9 18.2 %all_to_all.32 = bf16[128,16,128]{2,1,0:T(8,128)(2,1)} all-to-all(bf16[128,16,128]{2,1,0:T(8,128)(2,1)S(1)} %copy.38), channel_id=1, replica_groups=mesh['row'=16,'col'=8] {'row','col'}, dimensions={0} | all-to-all | bytes 1048576 | tf_op jit(solution)/shard_map/all_to_all | solution.py:17
  109.1 1.6 reshape.191
  112.2 1.9 reshape.192
  114.2 2.3 %convolution_convert_fusion = bf16[512,512]{1,0:T(8,128)(2,1)} fusion(bf16[512,512]{1,0:T(8,128)(2,1)S(1)} %reshape.192, bf16[512,512]{1,0:T(8,128)(2,1)} %copy-done.14), kind=kOutput, calls=%fused_computation.10 | convolution fusion | flops 268697600 | bytes 1572864 | tf_op jit(solution)/shard_map/ij,ik->jk/dot_general | solution.py:62
  117.7 1.6 reshape.193
  120.5 2.4 %stack_reshape.14 = bf16[128,1,16,128]{3,2,0,1:T(8,128)(2,1)} reshape(bf16[16,8,32,64]{3,2,1,0:T(8,128)(2,1)} %bitcast.156) | data formatting | bytes 1048576 | tf_op jit(solution)/shard_map/stack;reshape | solution.py:102
  125.8 1.8 stack_reshape.15
  129.9 6.0 %all-to-all-start.3 = ((bf16[128,2,16,128]{3,2,1,0:T(8,128)(2,1)}), bf16[128,2,16,128]{3,2,1,0:T(8,128)(2,1)}, u32[]{:S(2)}, u32[]{:S(2)}) async-start(bf16[128,2,16,128]{3,2,1,0:T(8,128)(2,1)} %copy.42), calls=%async_computation.3 | async-start | bytes 2097152 | tf_op jit(solution)/shard_map/all_to_all | solution.py:17
  136.2 2.2 %fusion.47 = f32[128,128]{1,0:T(8,128)} fusion(bf16[128,2048]{0,1:T(8,128)(2,1)} %copy-done.13, bf16[128,2048]{0,1:T(8,128)(2,1)} %copy-done.11), kind=kOutput, calls=%fused_computation.102 | convolution fusion | flops 67108864 | bytes 1114112 | tf_op jit(solution)/shard_map/hp,cp->hc/dot_general | solution.py:62
  138.4 2.2 %fusion.46 = f32[128,128]{1,0:T(8,128)} fusion(bf16[2048,128]{1,0:T(8,128)(2,1)} %bitcast.148, bf16[128,2048]{0,1:T(8,128)(2,1)} %get-tuple-element.18), kind=kOutput, calls=%fused_computation.101 | convolution fusion | flops 67108864 | bytes 1114112 | tf_op jit(solution)/shard_map/pc,dp->cd/dot_general | solution.py:62
  140.5 13.3 %all-to-all-done.3 = bf16[128,2,16,128]{3,2,1,0:T(8,128)(2,1)} async-done(((bf16[128,2,16,128]{3,2,1,0:T(8,128)(2,1)}), bf16[128,2,16,128]{3,2,1,0:T(8,128)(2,1)}, u32[]{:S(2)}, u32[]{:S(2)}) %all-to-all-start.3) | async-done | bytes 1048608 | tf_op jit(solution)/shard_map/all_to_all | solution.py:17
  153.8 2.7 %slice_convert_fusion.1 = (f32[128,1,16,128]{3,2,1,0:T(8,128)}, f32[128,1,16,128]{3,2,1,0:T(8,128)}) fusion(bf16[128,2,16,128]{3,2,1,0:T(8,128)(2,1)} %all-to-all-done.3), kind=kLoop, calls=%fused_computation.75 | loop fusion | flops 524288 | bytes 3145728 | tf_op jit(solution)/shard_map/convert_element_type | solution.py:103
  158.1 2.6 %copy.44 = f32[128,1,16,128]{0,3,2,1:T(8,128)} copy(f32[128,1,16,128]{3,2,1,0:T(8,128)} %get-tuple-element.21) | data formatting | bytes 2097152 | tf_op jit(solution)/shard_map/convert_element_type | solution.py:104
  160.6 2.4 %multiply_convert_fusion.3 = (bf16[128,2048]{0,1:T(8,128)(2,1)S(1)}, bf16[128,2048]{0,1:T(8,128)(2,1)S(1)}, bf16[128,2048]{0,1:T(8,128)(2,1)S(1)}, bf16[128,2048]{0,1:T(8,128)(2,1)S(1)}) fusion(f32[128,1,16,128]{0,3,2,1:T(8,128)S(1)} %copy.43, f32[2048]{0:T(1024)S(1)} %reshape.202, f32[256,2048]{0,1:T(8,128)} %copy-done.1, ...), kind=kLoop, calls=%fused_computation.61 | loop fusion | flops 5767168 | bytes 8396800 | tf_op jit(solution)/shard_map/convert.8
  165.7 2.3 %fusion.42 = (f32[128]{0:T(128)}, f32[2048]{0:T(1024)S(1)}, f32[2048,128]{1,0:T(8,128)S(1)}) fusion(f32[128]{0:T(128)S(1)} %copy-done.21, f32[2048,128]{1,0:T(8,128)S(1)} %fusion.34, f32[2048,128]{1,0:T(8,128)} %fusion.36, bf16[128,2048]{0,1:T(8,128)(2,1)S(1)} %copy-done.12, bf16[128,128]{1,0:T(8,128)(2,1)S(1)} %copy-done.20), kind=kOutput, calls=%fused_computation.97 | convolution fusion | flops 68417408 | bytes 3712000 | tf_op jit(solution)/shard_map/dp,cd->pc/dot_general | solution.py:62
  169.2 18.5 %all_to_all.33 = f32[128,8,128]{2,1,0:T(8,128)S(1)} all-to-all(f32[128,8,128]{2,1,0:T(8,128)S(1)} %pad_bitcast_fusion), channel_id=1, replica_groups=mesh['row'=16,'col'=8] {'row','col'}, dimensions={0} | all-to-all | bytes 1048576 | tf_op jit(solution)/shard_map/all_to_all | solution.py:17
  188.7 4.9 %all-to-all-start.5 = ((f32[128,8,128]{2,1,0:T(8,128)}), f32[128,8,128]{2,1,0:T(8,128)S(1)}, u32[]{:S(2)}, u32[]{:S(2)}) async-start(f32[128,8,128]{2,1,0:T(8,128)} %stack.20), calls=%async_computation.5 | async-start | bytes 1048576 | tf_op jit(solution)/shard_map/all_to_all | solution.py:140
  193.7 1.9 fusion.15
  195.6 11.4 %all-to-all-done.5 = f32[128,8,128]{2,1,0:T(8,128)S(1)} async-done(((f32[128,8,128]{2,1,0:T(8,128)}), f32[128,8,128]{2,1,0:T(8,128)S(1)}, u32[]{:S(2)}, u32[]{:S(2)}) %all-to-all-start.5) | async-done | bytes 524320 | tf_op jit(solution)/shard_map/all_to_all | solution.py:140
  (109 shorter events, 38.1 us)
Async XLA Ops:
  0.6 5.7 %copy-start = (bf16[128,256]{1,0:T(8,128)(2,1)S(1)}, bf16[128,256]{1,0:T(8,128)(2,1)}, u32[]{:S(2)}) copy-start(bf16[128,256]{1,0:T(8,128)(2,1)} %param.17) | copy-start | bytes 196612
  2.9 4.2 %copy-start.18 = (bf16[128,256]{1,0:T(8,128)(2,1)S(1)}, bf16[128,256]{1,0:T(8,128)(2,1)}, u32[]{:S(2)}) copy-start(bf16[128,256]{1,0:T(8,128)(2,1)} %param.16) | copy-start | bytes 196612
  6.3 0.8 copy-start.6
  7.6 1.3 copy-start.1
  47.3 7.2 %copy-start.9 = (bf16[512,512]{1,0:T(8,128)(2,1)}, bf16[512,512]{1,0:T(8,128)(2,1)S(1)}, u32[]{:S(2)}) copy-start(bf16[512,512]{1,0:T(8,128)(2,1)S(1)} %reshape.186) | copy-start | bytes 1572868
  54.5 0.8 copy-start.14
  61.2 20.8 %copy-start.22 = (f32[128]{0:T(128)S(1)}, f32[128]{0:T(128)}, u32[]{:S(2)}) copy-start(f32[128]{0:T(128)} %param.19) | copy-start | bytes 1540
  61.2 20.8 %copy-start.25 = (f32[128]{0:T(128)S(1)}, f32[128]{0:T(128)}, u32[]{:S(2)}) copy-start(f32[128]{0:T(128)} %param.20) | copy-start | bytes 1540
  79.7 0.8 copy-start.5
  79.7 2.9 %copy-start.19 = (bf16[128,128]{1,0:T(8,128)(2,1)S(1)}, bf16[128,128]{1,0:T(8,128)(2,1)}, u32[]{:S(2)}) copy-start(bf16[128,128]{1,0:T(8,128)(2,1)} %param.21) | copy-start | bytes 98308
  80.5 2.4 %copy-start.20 = (bf16[128,128]{1,0:T(8,128)(2,1)S(1)}, bf16[128,128]{1,0:T(8,128)(2,1)}, u32[]{:S(2)}) copy-start(bf16[128,128]{1,0:T(8,128)(2,1)} %param.18) | copy-start | bytes 98308
  82.0 1.0 copy-start.7
  82.6 1.6 copy-start.13
  83.0 1.2 copy-start.15
  85.4 4.1 %copy-start.11 = (bf16[128,2048]{0,1:T(8,128)(2,1)}, bf16[128,2048]{0,1:T(8,128)(2,1)S(1)}, u32[]{:S(2)}) copy-start(bf16[128,2048]{0,1:T(8,128)(2,1)S(1)} %get-tuple-element.19) | copy-start | bytes 1572868
  87.0 2.4 %copy-start.3 = (f32[2048,128]{1,0:T(8,128)}, f32[2048,128]{1,0:T(8,128)S(1)}, u32[]{:S(2)}) copy-start(f32[2048,128]{1,0:T(8,128)S(1)} %get-tuple-element.36) | copy-start | bytes 3145732
  112.2 4.3 %copy-start.10 = (bf16[512,512]{1,0:T(8,128)(2,1)S(1)}, bf16[512,512]{1,0:T(8,128)(2,1)}, u32[]{:S(2)}) copy-start(bf16[512,512]{1,0:T(8,128)(2,1)} %copy-done.9) | copy-start | bytes 1572868
  128.8 7.1 %copy-start.4 = (f32[2048,128]{1,0:T(8,128)S(1)}, f32[2048,128]{1,0:T(8,128)}, u32[]{:S(2)}) copy-start(f32[2048,128]{1,0:T(8,128)} %copy-done.3) | copy-start | bytes 3145732
  129.9 23.9 %all-to-all-start.3 = ((bf16[128,2,16,128]{3,2,1,0:T(8,128)(2,1)}), bf16[128,2,16,128]{3,2,1,0:T(8,128)(2,1)}, u32[]{:S(2)}, u32[]{:S(2)}) async-start(bf16[128,2,16,128]{3,2,1,0:T(8,128)(2,1)} %copy.42), calls=%async_computation.3 | async-start | bytes 2097152 | tf_op jit(solution)/shard_map/all_to_all | solution.py:17
  160.6 2.4 %copy-start.8 = (bf16[32,64,128]{2,1,0:T(8,128)(2,1)S(1)}, bf16[32,64,128]{2,1,0:T(8,128)(2,1)}, u32[]{:S(2)}) copy-start(bf16[32,64,128]{2,1,0:T(8,128)(2,1)} %copy-done.6) | copy-start | bytes 1572868
  163.9 1.8 copy-start.12
  163.9 1.8 copy-start.21
  165.6 2.4 %copy-start.2 = (bf16[32,64,128]{2,1,0:T(8,128)(2,1)S(1)}, bf16[32,64,128]{2,1,0:T(8,128)(2,1)}, u32[]{:S(2)}) copy-start(bf16[32,64,128]{2,1,0:T(8,128)(2,1)} %param.11) | copy-start | bytes 1572868
  168.0 1.1 copy-start.16
  168.0 1.1 copy-start.17
  168.0 1.1 copy-start.23
  168.0 1.1 copy-start.24
  188.7 18.3 %all-to-all-start.5 = ((f32[128,8,128]{2,1,0:T(8,128)}), f32[128,8,128]{2,1,0:T(8,128)S(1)}, u32[]{:S(2)}, u32[]{:S(2)}) async-start(f32[128,8,128]{2,1,0:T(8,128)} %stack.20), calls=%async_computation.5 | async-start | bytes 1048576 | tf_op jit(solution)/shard_map/all_to_all | solution.py:140
